TPU v7x, 32 devices: a whole 2x2x4 slice. The times are simulated.
32 devices in a mesh: dp: 8 (over y, x, core), tensor: 4 (over z).
Axes of the slice: x: 2, y: 2, z: 4, core: 2. Of those that a mesh axis runs over, the one named last changes fastest.
Arguments:
- layer_input: float32 [16, 512, 2048], P('dp', 'tensor'), may hold values from -6 to 6
- segments: int32 [16, 512], P('dp'), may hold values from 0 to 7, never falling along the last dimension, each value on 1 to 256 neighbouring positions
- gain_attn: bfloat16 [2048], P('dp'), may hold values from 0.5 to 1.5
- w_qkv: bfloat16 [2048, 4, 640], P('dp', 'tensor'), as said below
- w_out_t: bfloat16 [2048, 2048], P('dp', 'tensor'), may hold values from -0.75 to 0.75
- gain_mlp: bfloat16 [2048], P('dp'), may hold values from 0.5 to 1.5
- w_gate_up: bfloat16 [2048, 2, 5632], P('dp', None, 'tensor'), may hold values from -0.125 to 0.125
- w_down_t: bfloat16 [2048, 5632], P('dp', 'tensor'), may hold values from -0.078125 to 0.078125
- cotangent: float32 [16, 512, 2048], P('dp', 'tensor'), may hold values from -6 to 6
Outputs:
- output: float32 [16, 512, 2048], P('dp', 'tensor')
- input_grad: float32 [16, 512, 2048], P('dp', 'tensor')
- gain_attn_grad: float32 [2048], P('dp')
- qkv_grad: float32 [2048, 4, 640], P('dp', 'tensor')
- out_grad: float32 [2048, 2048], P('dp', 'tensor')
- gain_mlp_grad: float32 [2048], P('dp')
- gate_up_grad: float32 [2048, 2, 5632], P('dp', None, 'tensor')
- down_grad: float32 [2048, 5632], P('dp', 'tensor')
Inputs may be any that keep to these rules, and one draw needn't show every extreme that they name: `w_qkv`: for each key-value group the columns hold the queries of its 8 heads, then its key, then its value.
All inputs are finite; a program needn't handle non-finite values.
Results may differ from a plain program's by a relative error of at most 0.013.
Values may be sent and summed in bfloat16 or wider, within the bound.
A program may use at most 256 MiB of HBM per device.

v0:
```python
import math
import jax
import jax.numpy as jnp
from jax import lax
from jax.sharding import PartitionSpec as P

H = 32
KV = 4
HD = 64
NORM_EPS = 1e-05


def rope_tables(segment_row, head_size):
    row_count = segment_row.shape[0]
    earlier = jnp.sum((segment_row[None, :] < segment_row[:, None]).astype(jnp.int32), axis=1)
    position = (jnp.arange(row_count, dtype=jnp.int32) - earlier).astype(jnp.float32)
    half_size = head_size // 2
    frequency = jnp.exp(
        jnp.arange(half_size, dtype=jnp.float32) * (-2.0 * math.log(10000.0) / head_size)
    )
    angles = position[:, None] * frequency[None, :]
    return (jnp.cos(angles), jnp.sin(angles))


def expand_table(angle_table, rank_count):
    return angle_table.reshape(
        (angle_table.shape[0],) + (1,) * (rank_count - 2) + (angle_table.shape[1],)
    )


def rotate(values, cosine, sine_tab):
    half_size = values.shape[-1] // 2
    cosine = expand_table(cosine, values.ndim)
    sine_tab = expand_table(sine_tab, values.ndim)
    first_half = values[..., :half_size]
    second_half = values[..., half_size:]
    return jnp.concatenate(
        [
            first_half * cosine - second_half * sine_tab,
            second_half * cosine + first_half * sine_tab,
        ],
        axis=-1,
    )


def unrotate(values, cosine, sine_tab):
    half_size = values.shape[-1] // 2
    cosine = expand_table(cosine, values.ndim)
    sine_tab = expand_table(sine_tab, values.ndim)
    first_half = values[..., :half_size]
    second_half = values[..., half_size:]
    return jnp.concatenate(
        [
            first_half * cosine + second_half * sine_tab,
            second_half * cosine - first_half * sine_tab,
        ],
        axis=-1,
    )


def allowed_pairs(segment_row):
    row_count = segment_row.shape[0]
    position = jnp.arange(row_count, dtype=jnp.int32)
    return (segment_row[:, None] == segment_row[None, :]) & (position[None, :] <= position[:, None])


def norm_forward(row_block, gain_row):
    inv_rms = lax.rsqrt(jnp.mean(row_block * row_block, axis=-1, keepdims=True) + NORM_EPS)
    return ((row_block * inv_rms * gain_row.astype(jnp.float32)).astype(jnp.bfloat16), inv_rms)


def norm_backward(row_block, inv_rms, gain_row, upstream):
    weighted = upstream * gain_row.astype(jnp.float32)
    back_term = inv_rms * weighted - row_block * (inv_rms * inv_rms * inv_rms) * jnp.mean(
        weighted * row_block, axis=-1, keepdims=True
    )
    return (back_term, jnp.sum(upstream * row_block * inv_rms, axis=0))


def split_heads(qkv_rows, head_group, head_size):
    row_count, groups = (qkv_rows.shape[0], qkv_rows.shape[1])
    query = qkv_rows[:, :, : head_group * head_size].reshape(
        row_count, groups, head_group, head_size
    )
    key_part = qkv_rows[:, :, head_group * head_size : (head_group + 1) * head_size]
    value_part = qkv_rows[:, :, (head_group + 1) * head_size :]
    return (query, key_part, value_part)


def score_block(query, key_part, allowed, head_size):
    scores = jnp.einsum("igne,jge->gnij", query, key_part, preferred_element_type=jnp.float32) * (
        1.0 / math.sqrt(head_size)
    )
    return jnp.where(allowed[None, None], scores, jnp.float32(-1e30))


def attend_forward(qkv_rows, segment_row, head_group, head_size):
    cosine, sine_tab = rope_tables(segment_row, head_size)
    query, key_part, value_part = split_heads(qkv_rows, head_group, head_size)
    query = rotate(query, cosine, sine_tab).astype(jnp.bfloat16)
    key_part = rotate(key_part, cosine, sine_tab).astype(jnp.bfloat16)
    value_part = value_part.astype(jnp.bfloat16)
    allowed = allowed_pairs(segment_row)
    scores = score_block(query, key_part, allowed, head_size)
    row_max = jnp.max(scores, axis=-1, keepdims=True)
    log_total = row_max + jnp.log(jnp.sum(jnp.exp(scores - row_max), axis=-1, keepdims=True))
    weights = jnp.exp(scores - log_total).astype(jnp.bfloat16)
    mixed = jnp.einsum("gnij,jge->igne", weights, value_part, preferred_element_type=jnp.float32)
    mixed = mixed.astype(jnp.bfloat16).reshape(qkv_rows.shape[0], -1)
    return (mixed, (query, key_part, value_part, log_total, cosine, sine_tab, allowed))


def attend_backward(grad_out, saved, head_size):
    query, key_part, value_part, log_total, cosine, sine_tab, allowed = saved
    row_count, groups, head_group = (query.shape[0], query.shape[1], query.shape[2])
    scores = score_block(query, key_part, allowed, head_size)
    weights = jnp.exp(scores - log_total)
    grad_heads = grad_out.reshape(row_count, groups, head_group, head_size)
    grad_value = jnp.einsum(
        "gnij,igne->jge",
        weights.astype(jnp.bfloat16),
        grad_heads,
        preferred_element_type=jnp.float32,
    )
    grad_weights = jnp.einsum(
        "igne,jge->gnij", grad_heads, value_part, preferred_element_type=jnp.float32
    )
    grad_scores = (
        weights
        * (grad_weights - jnp.sum(weights * grad_weights, axis=-1, keepdims=True))
        * (1.0 / math.sqrt(head_size))
    )
    grad_scores = grad_scores.astype(jnp.bfloat16)
    grad_query = jnp.einsum(
        "gnij,jge->igne", grad_scores, key_part, preferred_element_type=jnp.float32
    )
    grad_key = jnp.einsum("gnij,igne->jge", grad_scores, query, preferred_element_type=jnp.float32)
    grad_query = unrotate(grad_query, cosine, sine_tab).reshape(
        row_count, groups, head_group * head_size
    )
    grad_key = unrotate(grad_key, cosine, sine_tab)
    return jnp.concatenate([grad_query, grad_key, grad_value], axis=2).astype(jnp.bfloat16)


def outer_product(left_rows, right_rows):
    return lax.dot_general(
        left_rows, right_rows, (((0,), (0,)), ((), ())), preferred_element_type=jnp.float32
    )


def right_product(left_rows, right_matrix):
    return lax.dot_general(
        left_rows, right_matrix, (((1,), (1,)), ((), ())), preferred_element_type=jnp.float32
    )


def spread_forward(row_block):
    return lax.all_gather(row_block, "tensor", axis=0, tiled=True)


def spread_backward(row_block):
    return lax.all_gather(row_block, "tensor", axis=0, tiled=True)


def branch_sum(term_fn, local_rows):
    return lax.psum_scatter(
        term_fn(jnp.int32(0), lax.axis_size("tensor") * local_rows),
        "tensor",
        scatter_dimension=0,
        tiled=True,
    )


def input_sum(term_fn, local_rows):
    return lax.psum_scatter(
        term_fn(jnp.int32(0), lax.axis_size("tensor") * local_rows),
        "tensor",
        scatter_dimension=0,
        tiled=True,
    )


def add_terms(left_terms, right_terms):
    if left_terms is None:
        return right_terms
    return tuple((left_term + right_term for left_term, right_term in zip(left_terms, right_terms)))


def body(
    layer_input, segments, gain_attn, w_qkv, w_out_t, gain_mlp, w_gate_up, w_down_t, cotangent
):
    head_group = H // KV
    weight_shard = (gain_attn, w_qkv, w_out_t, gain_mlp, w_gate_up, w_down_t)
    local_rows = layer_input.shape[1]
    outputs = []
    input_grads = []
    grad_total = None
    owned_grads = None
    for number in range(layer_input.shape[0]):
        gathered_weights = (
            lax.all_gather(weight_shard[0], "dp", axis=0, tiled=True),
            lax.all_gather(weight_shard[1], "dp", axis=0, tiled=True),
            lax.all_gather(weight_shard[2], "dp", axis=0, tiled=True),
            lax.all_gather(weight_shard[3], "dp", axis=0, tiled=True),
            lax.all_gather(weight_shard[4], "dp", axis=0, tiled=True),
            lax.all_gather(weight_shard[5], "dp", axis=0, tiled=True),
        )
        g_attn, qkv_w, out_w, g_mlp, gu_w, down_w = gathered_weights
        model_width = qkv_w.shape[0]
        groups = qkv_w.shape[1]
        hidden_width = gu_w.shape[2]
        segment_row = segments[number]
        rows_in = layer_input[number]
        normed_attn, scale_attn = norm_forward(rows_in, g_attn)
        gathered_attn = spread_forward(normed_attn)
        row_count = gathered_attn.shape[0]
        qkv_rows = jnp.dot(
            gathered_attn, qkv_w.reshape(model_width, -1), preferred_element_type=jnp.float32
        ).reshape(row_count, groups, -1)
        mixed, saved = attend_forward(qkv_rows, segment_row, head_group, HD)

        def attn_term(row_start, row_span):
            return right_product(mixed, out_w)

        residual = rows_in + branch_sum(attn_term, local_rows)
        normed_mlp, scale_mlp = norm_forward(residual, g_mlp)
        gathered_mlp = spread_forward(normed_mlp)
        gate_up = jnp.dot(
            gathered_mlp, gu_w.reshape(model_width, -1), preferred_element_type=jnp.float32
        ).reshape(row_count, 2, hidden_width)
        gate_part = gate_up[:, 0]
        up_part = gate_up[:, 1]
        sigmoid_gate = jax.nn.sigmoid(gate_part)
        active = gate_part * sigmoid_gate
        hidden = (active * up_part).astype(jnp.bfloat16)

        def mlp_term(row_start, row_span):
            return right_product(hidden, down_w)

        outputs.append(residual + branch_sum(mlp_term, local_rows))
        back_weights = (
            lax.all_gather(weight_shard[0], "dp", axis=0, tiled=True),
            lax.all_gather(weight_shard[1], "dp", axis=0, tiled=True),
            lax.all_gather(weight_shard[2], "dp", axis=0, tiled=True),
            lax.all_gather(weight_shard[3], "dp", axis=0, tiled=True),
            lax.all_gather(weight_shard[4], "dp", axis=0, tiled=True),
            lax.all_gather(weight_shard[5], "dp", axis=0, tiled=True),
        )
        g_attn, qkv_w, out_w, g_mlp, gu_w, down_w = back_weights
        grad_in = cotangent[number]
        grad_rows = spread_backward(grad_in.astype(jnp.bfloat16))
        grad_down = outer_product(grad_rows, hidden)
        grad_hidden = jnp.dot(grad_rows, down_w, preferred_element_type=jnp.float32)
        grad_gu = jnp.stack(
            [
                grad_hidden * up_part * sigmoid_gate * (1.0 + gate_part * (1.0 - sigmoid_gate)),
                grad_hidden * active,
            ],
            axis=1,
        ).astype(jnp.bfloat16)
        flat_gu = grad_gu.reshape(row_count, -1)
        grad_gu_w = outer_product(gathered_mlp, flat_gu).reshape(model_width, 2, hidden_width)
        gu_flat = gu_w.reshape(model_width, -1)

        def mlp_back(row_start, row_span):
            return right_product(flat_gu, gu_flat)

        grad_normed_mlp = input_sum(mlp_back, local_rows)
        back_mlp, grad_g_mlp = norm_backward(residual, scale_mlp, g_mlp, grad_normed_mlp)
        grad_resid = grad_in + back_mlp
        resid_rows = spread_backward(grad_resid.astype(jnp.bfloat16))
        grad_out_w = outer_product(resid_rows, mixed)
        grad_mixed = jnp.dot(resid_rows, out_w, preferred_element_type=jnp.float32).astype(
            jnp.bfloat16
        )
        grad_qkv = attend_backward(grad_mixed, saved, HD)
        flat_qkv = grad_qkv.reshape(row_count, -1)
        grad_qkv_w = outer_product(gathered_attn, flat_qkv).reshape(qkv_w.shape)
        qkv_flat = qkv_w.reshape(model_width, -1)

        def attn_back(row_start, row_span):
            return right_product(flat_qkv, qkv_flat)

        grad_normed_attn = input_sum(attn_back, local_rows)
        back_attn, grad_g_attn = norm_backward(rows_in, scale_attn, g_attn, grad_normed_attn)
        input_grads.append(grad_resid + back_attn)
        grad_terms = (grad_g_attn, grad_qkv_w, grad_out_w, grad_g_mlp, grad_gu_w, grad_down)
        grad_total = add_terms(grad_total, grad_terms)
    owned_grads = lax.psum_scatter(grad_total, "dp", scatter_dimension=0, tiled=True)
    gain_first, gain_second = lax.psum((owned_grads[0], owned_grads[3]), "tensor")
    return (
        jnp.stack(outputs),
        jnp.stack(input_grads),
        gain_first,
        owned_grads[1],
        owned_grads[2],
        gain_second,
        owned_grads[4],
        owned_grads[5],
    )


def solution(mesh):
    placed = (
        P("dp", "tensor", None),
        P("dp", None),
        P("dp"),
        P("dp", "tensor", None),
        P("dp", "tensor"),
        P("dp"),
        P("dp", None, "tensor"),
        P("dp", "tensor"),
        P("dp", "tensor", None),
    )
    return jax.shard_map(
        body,
        mesh=mesh,
        in_specs=placed,
        out_specs=(
            P("dp", "tensor", None),
            P("dp", "tensor", None),
            P("dp"),
            P("dp", "tensor", None),
            P("dp", "tensor"),
            P("dp"),
            P("dp", None, "tensor"),
            P("dp", "tensor"),
        ),
        check_vma=False,
    )
```

profile of v0, /device:TPU:0, one launch (start us, length us, event | category | flops | bytes accessed | tf_op | source)
XLA Modules:
  0.0 1613.4 jit_solution(4839132049116461535)
XLA Ops:
  9.8 10.4 all-gather
  26.1 42.1 %all-gather.15.cloned.1.call-done = bf16[512,2048]{1,0:T(8,128)(2,1)} async-done(((bf16[128,2048]{1,0:T(8,128)(2,1)}), bf16[512,2048]{1,0:T(8,128)(2,1)}) %all-gather.15.cloned.1.call-update) | async-done | bytes 2097168 | tf_op jit(solution)/shard_map/all_gather | solution.py:158
  68.2 30.7 %all-gather.17.cloned.1.call-done = bf16[2048,1,640]{2,0,1:T(8,128)(2,1)} async-done(((bf16[256,1,640]{2,0,1:T(8,128)(2,1)}), bf16[2048,1,640]{2,0,1:T(8,128)(2,1)}) %all-gather.17.cloned.1.call-update) | async-done | bytes 2621456 | tf_op jit(solution)/shard_map/all_gather | solution.py:202
  105.6 41.1 %all-gather.27.cloned.1.call-done = bf16[512,2048]{1,0:T(8,128)(2,1)} async-done(((bf16[128,2048]{1,0:T(8,128)(2,1)}), bf16[512,2048]{1,0:T(8,128)(2,1)}) %all-gather.27.cloned.1.call-update) | async-done | bytes 2097168 | tf_op jit(solution)/shard_map/all_gather | solution.py:158
  161.5 13.6 all-gather.19.cloned.1.call-done
  210.8 46.2 %reduce-scatter.13.cloned.1.call-done = f32[128,2048]{1,0:T(8,128)} async-done(((f32[512,2048]{1,0:T(8,128)}), f32[128,2048]{1,0:T(8,128)}) %reduce-scatter.13.cloned.1.call-update) | async-done | bytes 1048592 | tf_op jit(solution)/shard_map/reduce_scatter | solution.py:166
  257.0 79.5 %reduce-scatter.17.cloned.1.call-done = f32[128,2048]{1,0:T(8,128)} async-done(((f32[512,2048]{1,0:T(8,128)}), f32[128,2048]{1,0:T(8,128)}) %reduce-scatter.17.cloned.1.call-update) | async-done | bytes 1048592 | tf_op jit(solution)/shard_map/reduce_scatter | solution.py:166
  343.9 63.1 %all-gather.23.cloned.1.call-done = bf16[2048,2,1408]{2,0,1:T(8,128)(2,1)} async-done(((bf16[256,2,1408]{2,0,1:T(8,128)(2,1)}), bf16[2048,2,1408]{2,0,1:T(8,128)(2,1)}) %all-gather.23.cloned.1.call-update) | async-done | bytes 11534352 | tf_op jit(solution)/shard_map/all_gather | solution.py:205
  407.0 15.2 copy.87
  422.2 32.6 %all-gather.21.cloned.1.call-done = bf16[512,2048]{1,0:T(8,128)(2,1)} async-done(((bf16[128,2048]{1,0:T(8,128)(2,1)}), bf16[512,2048]{1,0:T(8,128)(2,1)}) %all-gather.21.cloned.1.call-update) | async-done | bytes 2097168 | tf_op jit(solution)/shard_map/all_gather | solution.py:158
  454.8 11.8 fusion.2
  466.6 34.8 %all-gather.31.cloned.1.call-done = bf16[512,2048]{1,0:T(8,128)(2,1)} async-done(((bf16[128,2048]{1,0:T(8,128)(2,1)}), bf16[512,2048]{1,0:T(8,128)(2,1)}) %all-gather.31.cloned.1.call-update) | async-done | bytes 2097168 | tf_op jit(solution)/shard_map/all_gather | solution.py:162
  501.5 43.8 %all-gather.25.cloned.1.call-done = bf16[2048,1408]{1,0:T(8,128)(2,1)} async-done(((bf16[256,1408]{1,0:T(8,128)(2,1)}), bf16[2048,1408]{1,0:T(8,128)(2,1)}) %all-gather.25.cloned.1.call-update) | async-done | bytes 5767184 | tf_op jit(solution)/shard_map/all_gather | solution.py:206
  566.2 76.9 %reduce-scatter.21.cloned.1.call-done = f32[128,2048]{1,0:T(8,128)} async-done(((f32[512,2048]{1,0:T(8,128)}), f32[128,2048]{1,0:T(8,128)}) %reduce-scatter.21.cloned.1.call-update) | async-done | bytes 1048592 | tf_op jit(solution)/shard_map/reduce_scatter | solution.py:175
  647.0 45.4 %all-gather.29.cloned.1.call-done = bf16[512,2048]{1,0:T(8,128)(2,1)} async-done(((bf16[128,2048]{1,0:T(8,128)(2,1)}), bf16[512,2048]{1,0:T(8,128)(2,1)}) %all-gather.29.cloned.1.call-update) | async-done | bytes 2097168 | tf_op jit(solution)/shard_map/all_gather | solution.py:158
  692.4 11.8 fusion
  704.2 34.9 %all-gather.35.cloned.1.call-done = bf16[512,2048]{1,0:T(8,128)(2,1)} async-done(((bf16[128,2048]{1,0:T(8,128)(2,1)}), bf16[512,2048]{1,0:T(8,128)(2,1)}) %all-gather.35.cloned.1.call-update) | async-done | bytes 2097168 | tf_op jit(solution)/shard_map/all_gather | solution.py:162
  749.6 10.3 convolution_bitcast_fusion
  785.5 50.3 %reduce-scatter.25.cloned.1.call-done = f32[128,2048]{1,0:T(8,128)} async-done(((f32[512,2048]{1,0:T(8,128)}), f32[128,2048]{1,0:T(8,128)}) %reduce-scatter.25.cloned.1.call-update) | async-done | bytes 1048592 | tf_op jit(solution)/shard_map/reduce_scatter | solution.py:175
  837.3 78.0 %reduce-scatter.15.cloned.1.call-done = f32[128,2048]{1,0:T(8,128)} async-done(((f32[512,2048]{1,0:T(8,128)}), f32[128,2048]{1,0:T(8,128)}) %reduce-scatter.15.cloned.1.call-update) | async-done | bytes 1048592 | tf_op jit(solution)/shard_map/reduce_scatter | solution.py:166
  915.2 79.5 %reduce-scatter.19.cloned.1.call-done = f32[128,2048]{1,0:T(8,128)} async-done(((f32[512,2048]{1,0:T(8,128)}), f32[128,2048]{1,0:T(8,128)}) %reduce-scatter.19.cloned.1.call-update) | async-done | bytes 1048592 | tf_op jit(solution)/shard_map/reduce_scatter | solution.py:166
  1012.7 33.7 %all-gather.33.cloned.1.call-done = bf16[512,2048]{1,0:T(8,128)(2,1)} async-done(((bf16[128,2048]{1,0:T(8,128)(2,1)}), bf16[512,2048]{1,0:T(8,128)(2,1)}) %all-gather.33.cloned.1.call-update) | async-done | bytes 2097168 | tf_op jit(solution)/shard_map/all_gather | solution.py:162
  1061.9 31.0 %all-gather.37.cloned.1.call-done = bf16[512,2048]{1,0:T(8,128)(2,1)} async-done(((bf16[128,2048]{1,0:T(8,128)(2,1)}), bf16[512,2048]{1,0:T(8,128)(2,1)}) %all-gather.37.cloned.1.call-update) | async-done | bytes 2097168 | tf_op jit(solution)/shard_map/all_gather | solution.py:162
  1145.3 13.4 fusion.21
  1161.7 17.7 %convolution_add_fusion = f32[2048,2,1408]{2,0,1:T(8,128)} fusion(f32[2048,2,1408]{2,0,1:T(8,128)} %fusion.21, bf16[512,2,1408]{0,2,1:T(8,128)(2,1)} %copy.110, bf16[512,2048]{1,0:T(8,128)(2,1)} %all-gather.29.cloned.1.call-done), kind=kOutput, calls=%fused_computation | convolution fusion | flops 5911347200 | bytes 51118080 | tf_op jit(solution)/shard_map/dot_general | solution.py:146
  1193.3 48.5 %reduce-scatter.29.cloned.1.call-done = f32[256,1,640]{2,0,1:T(8,128)} async-done(((f32[2048,1,640]{2,0,1:T(8,128)}), f32[256,1,640]{2,0,1:T(8,128)}) %reduce-scatter.29.cloned.1.call-update) | async-done | bytes 655376 | tf_op jit(solution)/shard_map/reduce_scatter | solution.py:289
  1244.4 76.5 %reduce-scatter.27.cloned.1.call-done = f32[128,2048]{1,0:T(8,128)} async-done(((f32[512,2048]{1,0:T(8,128)}), f32[128,2048]{1,0:T(8,128)}) %reduce-scatter.27.cloned.1.call-update) | async-done | bytes 1048592 | tf_op jit(solution)/shard_map/reduce_scatter | solution.py:175
  1320.9 79.6 %reduce-scatter.23.cloned.1.call-done = f32[128,2048]{1,0:T(8,128)} async-done(((f32[512,2048]{1,0:T(8,128)}), f32[128,2048]{1,0:T(8,128)}) %reduce-scatter.23.cloned.1.call-update) | async-done | bytes 1048592 | tf_op jit(solution)/shard_map/reduce_scatter | solution.py:175
  1402.7 23.7 %all-reduce.2 = (f32[2048]{0:T(1024)S(1)}, f32[2048]{0:T(1024)S(1)}) all-reduce(f32[2048]{0:T(1024)S(1)} %add.202, f32[2048]{0:T(1024)S(1)} %add.206), channel_id=10, replica_groups=mesh['dp'=8,'tensor'=4] {'dp'}, use_global_device_ids=true, to_apply=%region_26.27.clone | all-reduce | flops 4096 | bytes 32768
  1426.5 12.0 all-reduce.3
  1442.4 108.7 %reduce-scatter.33.cloned.1.call-done = f32[256,2,1408]{2,0,1:T(8,128)} async-done(((f32[2048,2,1408]{2,0,1:T(8,128)}), f32[256,2,1408]{2,0,1:T(8,128)}) %reduce-scatter.33.cloned.1.call-update) | async-done | bytes 2883600 | tf_op jit(solution)/shard_map/reduce_scatter | solution.py:289
  1556.7 49.4 %reduce-scatter.31.cloned.1.call-done = f32[256,512]{1,0:T(8,128)} async-done(((f32[2048,512]{1,0:T(8,128)}), f32[256,512]{1,0:T(8,128)}) %reduce-scatter.31.cloned.1.call-update) | async-done | bytes 524304 | tf_op jit(solution)/shard_map/reduce_scatter | solution.py:289
  (341 shorter events, 250.5 us)
Async XLA Ops:
  7.2 61.0 %all-gather.15.cloned.1.call-start = ((), (), s32[]{:S(2)}) async-start(), calls=%async_computation.12 | async-start | bytes 2621440 | tf_op jit(solution)/shard_map/all_gather | solution.py:158
  22.1 76.8 %all-gather.17.cloned.1.call-start = ((), (), s32[]{:S(2)}) async-start(), calls=%async_computation.13 | async-start | bytes 2949120 | tf_op jit(solution)/shard_map/all_gather | solution.py:202
  22.9 123.9 %all-gather.27.cloned.1.call-start = ((), (), s32[]{:S(2)}) async-start(), calls=%async_computation.20 | async-start | bytes 2621440 | tf_op jit(solution)/shard_map/all_gather | solution.py:158
  23.6 151.5 %all-gather.19.cloned.1.call-start = ((), (), s32[]{:S(2)}) async-start(), calls=%async_computation.14 | async-start | bytes 2359296 | tf_op jit(solution)/shard_map/all_gather | solution.py:203
  24.2 232.8 %reduce-scatter.13.cloned.1.call-start = ((), (), s32[]{:S(2)}) async-start(), calls=%async_computation.15 | async-start | bytes 5242880 | tf_op jit(solution)/shard_map/reduce_scatter | solution.py:166
  24.8 126.2 %copy-start.70 = (f32[512]{0:T(512)}, f32[512]{0:T(512)S(1)}, u32[]{:S(2)}) copy-start(f32[512]{0:T(512)S(1)} %get-tuple-element.119) | copy-start | bytes 6148
  180.0 156.4 %reduce-scatter.17.cloned.1.call-start = ((), (), s32[]{:S(2)}) async-start(), calls=%async_computation.21 | async-start | bytes 5242880 | tf_op jit(solution)/shard_map/reduce_scatter | solution.py:166
  199.1 207.9 %all-gather.23.cloned.1.call-start = ((), (), s32[]{:S(2)}) async-start(), calls=%async_computation.17 | async-start | bytes 12976128 | tf_op jit(solution)/shard_map/all_gather | solution.py:205
  201.8 253.0 %all-gather.21.cloned.1.call-start = ((), (), s32[]{:S(2)}) async-start(), calls=%async_computation.16 | async-start | bytes 2621440 | tf_op jit(solution)/shard_map/all_gather | solution.py:158
  340.2 161.3 %all-gather.31.cloned.1.call-start = ((), (), s32[]{:S(2)}) async-start(), calls=%async_computation.24 | async-start | bytes 2621440 | tf_op jit(solution)/shard_map/all_gather | solution.py:162
  342.9 202.4 %all-gather.25.cloned.1.call-start = ((), (), s32[]{:S(2)}) async-start(), calls=%async_computation.18 | async-start | bytes 6488064 | tf_op jit(solution)/shard_map/all_gather | solution.py:206
  343.5 299.6 %reduce-scatter.21.cloned.1.call-start = ((), (), s32[]{:S(2)}) async-start(), calls=%async_computation.25 | async-start | bytes 5242880 | tf_op jit(solution)/shard_map/reduce_scatter | solution.py:175
  566.1 126.3 %all-gather.29.cloned.1.call-start = ((), (), s32[]{:S(2)}) async-start(), calls=%async_computation.22 | async-start | bytes 2621440 | tf_op jit(solution)/shard_map/all_gather | solution.py:158
  646.1 93.0 %all-gather.35.cloned.1.call-start = ((), (), s32[]{:S(2)}) async-start(), calls=%async_computation.28 | async-start | bytes 2621440 | tf_op jit(solution)/shard_map/all_gather | solution.py:162
  646.8 188.9 %reduce-scatter.25.cloned.1.call-start = ((), (), s32[]{:S(2)}) async-start(), calls=%async_computation.29 | async-start | bytes 5242880 | tf_op jit(solution)/shard_map/reduce_scatter | solution.py:175
  760.0 155.2 %reduce-scatter.15.cloned.1.call-start = ((), (), s32[]{:S(2)}) async-start(), calls=%async_computation.19 | async-start | bytes 5242880 | tf_op jit(solution)/shard_map/reduce_scatter | solution.py:166
  772.7 222.0 %reduce-scatter.19.cloned.1.call-start = ((), (), s32[]{:S(2)}) async-start(), calls=%async_computation.23 | async-start | bytes 5242880 | tf_op jit(solution)/shard_map/reduce_scatter | solution.py:166
  785.4 209.3 %copy-start.15 = (f32[128,2048]{1,0:T(8,128)S(1)}, f32[128,2048]{1,0:T(8,128)}, u32[]{:S(2)}) copy-start(f32[128,2048]{1,0:T(8,128)} %reduce-scatter.21.cloned.1.call-done) | copy-start | bytes 3145732
  785.4 261.0 %all-gather.33.cloned.1.call-start = ((), (), s32[]{:S(2)}) async-start(), calls=%async_computation.26 | async-start | bytes 2621440 | tf_op jit(solution)/shard_map/all_gather | solution.py:162
  1000.1 92.8 %all-gather.37.cloned.1.call-start = ((), (), s32[]{:S(2)}) async-start(), calls=%async_computation.30 | async-start | bytes 2621440 | tf_op jit(solution)/shard_map/all_gather | solution.py:162
  1000.7 189.6 %reduce-scatter.35.cloned.1.call-start = ((), (), s32[]{:S(2)}) async-start(), calls=%async_computation.35 | async-start | bytes 12976128 | tf_op jit(solution)/shard_map/reduce_scatter | solution.py:289
  1012.2 229.6 %reduce-scatter.29.cloned.1.call-start = ((), (), s32[]{:S(2)}) async-start(), calls=%async_computation.32 | async-start | bytes 5898240 | tf_op jit(solution)/shard_map/reduce_scatter | solution.py:289
  1128.9 192.0 %reduce-scatter.27.cloned.1.call-start = ((), (), s32[]{:S(2)}) async-start(), calls=%async_computation.31 | async-start | bytes 5242880 | tf_op jit(solution)/shard_map/reduce_scatter | solution.py:175
  1134.5 266.0 %reduce-scatter.23.cloned.1.call-start = ((), (), s32[]{:S(2)}) async-start(), calls=%async_computation.27 | async-start | bytes 5242880 | tf_op jit(solution)/shard_map/reduce_scatter | solution.py:175
  1140.4 410.7 %reduce-scatter.33.cloned.1.call-start = ((), (), s32[]{:S(2)}) async-start(), calls=%async_computation.34 | async-start | bytes 25952256 | tf_op jit(solution)/shard_map/reduce_scatter | solution.py:289
  1179.5 426.6 %reduce-scatter.31.cloned.1.call-start = ((), (), s32[]{:S(2)}) async-start(), calls=%async_computation.33 | async-start | bytes 4718592 | tf_op jit(solution)/shard_map/reduce_scatter | solution.py:289
  1190.2 210.4 %copy-start.3 = (f32[2,128,2048]{2,1,0:T(8,128)S(1)}, f32[2,128,2048]{2,1,0:T(8,128)}, u32[]{:S(2)}) copy-start(f32[2,128,2048]{2,1,0:T(8,128)} %param.9) | copy-start | bytes 6291460
  1190.2 210.4 %copy-start.67 = (f32[8,1,256]{2,1,0:T(1,128)S(1)}, f32[8,1,256]{2,1,0:T(1,128)}, u32[]{:S(2)}) copy-start(f32[8,1,256]{2,1,0:T(1,128)} %copy-done.66) | copy-start | bytes 24580
  1190.2 210.4 %copy-start.76 = (f32[128]{0:T(128)S(1)}, f32[128]{0:T(128)}, u32[]{:S(2)}) copy-start(f32[128]{0:T(128)} %copy-done.75) | copy-start | bytes 1540
  1190.2 210.4 %copy-start.78 = (f32[128]{0:T(128)S(1)}, f32[128]{0:T(128)}, u32[]{:S(2)}) copy-start(f32[128]{0:T(128)} %copy-done.77) | copy-start | bytes 1540
  1193.3 245.2 %copy-start.82 = (f32[128]{0:T(128)S(1)}, f32[128]{0:T(128)}, u32[]{:S(2)}) copy-start(f32[128]{0:T(128)} %get-tuple-element.97) | copy-start | bytes 1540
  1193.3 245.2 %copy-start.83 = (f32[128]{0:T(128)S(1)}, f32[128]{0:T(128)}, u32[]{:S(2)}) copy-start(f32[128]{0:T(128)} %get-tuple-element.118) | copy-start | bytes 1540
  (86 other events, 1031.7 us)
Sparse Core Ops, SparseCore 0:
  22.2 45.9 all-gather.14
  70.1 28.7 all-gather.16
  101.1 45.6 all-gather.26
  148.5 26.5 all-gather.18
  180.1 76.7 reduce-scatter.12
  259.1 77.2 reduce-scatter.16
  338.9 68.0 all-gather.22
  409.2 45.6 all-gather.20
  457.0 44.4 all-gather.30
  503.2 41.9 all-gather.24
  566.3 76.7 reduce-scatter.20
  646.2 46.1 all-gather.28
  694.5 44.4 all-gather.34
  760.1 75.5 reduce-scatter.24
  837.9 77.2 reduce-scatter.14
  917.4 77.2 reduce-scatter.18
  1000.2 46.1 all-gather.32
  1048.4 44.4 all-gather.36
  1096.4 85.6 reduce-scatter.34
  1185.3 56.4 reduce-scatter.28
  1244.1 76.7 reduce-scatter.26
  1323.2 77.2 reduce-scatter.22
  1404.2 146.8 reduce-scatter.32
  1554.9 51.1 reduce-scatter.30
where the time goes:
time: 1620 us; the launch traced here: 1610 us
  waiting for transfers between devices  1220 us (75%)
  matrix products  200 us (12%)
  local copies, waits for them, and re-layouts  62.7 us (4%)
  blocking collectives  55 us (3%)
  other arithmetic  52.8 us (3%)
  between operations  16.8 us (1%)
    reduce_scatter x4, waiting for transfers between devices, input_sum(): lax.psum_scatter(term_fn(jnp.int32(0), lax.axis_size('tensor') * local_ro...  283 us
    reduce_scatter x4, waiting for transfers between devices, branch_sum(): lax.psum_scatter(term_fn(jnp.int32(0), lax.axis_size('tensor') * local_ro...  283 us
    reduce_scatter x4, waiting for transfers between devices, body(): lax.psum_scatter(grad_total, 'dp', scatter_dimension=0, tiled=True)  207 us
    all_gather x4, waiting for transfers between devices, spread_forward(): return lax.all_gather(row_block, 'tensor', axis=0, tiled=True)  161 us
    all_gather x4, waiting for transfers between devices, spread_backward(): return lax.all_gather(row_block, 'tensor', axis=0, tiled=True)  134 us
    all_gather x1, waiting for transfers between devices, body(): lax.all_gather(weight_shard[4], 'dp', axis=0, tiled=True)  63.1 us
    dot_general x8, matrix products, right_product(): lax.dot_general(left_rows, right_matrix, (((1,), (1,)), ((), ())), prefer...  55.7 us
    dot_general x8, matrix products, outer_product(): lax.dot_general(left_rows, right_rows, (((0,), (0,)), ((), ())), preferre...  55.1 us
  transfers between devices with their start and end apart: 24, of which 23 were waited for; matrix products, arithmetic and copies ran while one was open for 15% of the time, Pallas kernels for 0%

commit v1 on v0

--- a/solution.py
+++ b/solution.py
@@ -155,7 +155,9 @@
 
 
 def spread_forward(row_block):
-    return lax.all_gather(row_block, "tensor", axis=0, tiled=True)
+    return jnp.concatenate(
+        lax.all_to_all(jnp.stack([row_block] * lax.axis_size("tensor")), "tensor", 0, 0), axis=0
+    )
 
 
 def spread_backward(row_block):

time: 1620 us -> 1550 us (0.957)
  waiting for transfers between devices: 1220 us -> 1080 us
  blocking collectives: 55 us -> 108 us
    all_gather x4 -> x0, waiting for transfers between devices: 161 us -> none  [spread_forward(): return lax.all_gather(row_block, 'tensor', axis=0, tiled=True)]
    all_to_all x0 -> x3, waiting for transfers between devices: none -> 120 us  [spread_forward(): lax.all_to_all(jnp.stack([row_block] * lax.axis_size('tensor')), 'tensor'...]
    all_to_all x0 -> x1, blocking collectives: none -> 53.5 us  [spread_forward(): lax.all_to_all(jnp.stack([row_block] * lax.axis_size('tensor')), 'tensor'...]
    all_gather x4, waiting for transfers between devices: 134 us -> 85.4 us  [spread_backward(): return lax.all_gather(row_block, 'tensor', axis=0, tiled=True)]
    all_gather x1, waiting for transfers between devices: 30.7 us -> 0.01 us  [body(): lax.all_gather(weight_shard[1], 'dp', axis=0, tiled=True)]
    unnamed x197 -> x189, local copies, waits for them, and re-layouts: 32.6 us -> 32.4 us
  transfers between devices with their start and end apart: 24 -> 23, of which waited for: 23 -> 18; matrix products, arithmetic and copies ran while one was open for 15% -> 16% of each run, Pallas kernels for 0% -> 0%
where the time goes in v1:
time: 1550 us; the launch traced here: 1540 us
  waiting for transfers between devices  1080 us (70%)
  matrix products  202 us (13%)
  blocking collectives  108 us (7%)
  local copies, waits for them, and re-layouts  64.6 us (4%)
  other arithmetic  50 us (3%)
  between operations  16.7 us (1%)
  starting transfers between devices  15.8 us (1%)
    reduce_scatter x4, waiting for transfers between devices, input_sum(): lax.psum_scatter(term_fn(jnp.int32(0), lax.axis_size('tensor') * local_ro...  283 us
    reduce_scatter x4, waiting for transfers between devices, branch_sum(): lax.psum_scatter(term_fn(jnp.int32(0), lax.axis_size('tensor') * local_ro...  282 us
    reduce_scatter x4, waiting for transfers between devices, body(): lax.psum_scatter(grad_total, 'dp', scatter_dimension=0, tiled=True)  204 us
    all_to_all x3, waiting for transfers between devices, spread_forward(): lax.all_to_all(jnp.stack([row_block] * lax.axis_size('tensor')), 'tensor'...  120 us
    all_gather x4, waiting for transfers between devices, spread_backward(): return lax.all_gather(row_block, 'tensor', axis=0, tiled=True)  85.4 us
    all_gather x1, waiting for transfers between devices, body(): lax.all_gather(weight_shard[4], 'dp', axis=0, tiled=True)  61.3 us
    dot_general x8, matrix products, outer_product(): lax.dot_general(left_rows, right_rows, (((0,), (0,)), ((), ())), preferre...  56.3 us
    dot_general x8, matrix products, right_product(): lax.dot_general(left_rows, right_matrix, (((1,), (1,)), ((), ())), prefer...  55.8 us
  transfers between devices with their start and end apart: 23, of which 18 were waited for; matrix products, arithmetic and copies ran while one was open for 16% of the time, Pallas kernels for 0%

profile of v1, /device:TPU:0, one launch (start us, length us, event | category | flops | bytes accessed | tf_op | source)
XLA Modules:
  0.0 1539.9 jit_solution(15488686930300862107)
XLA Ops:
  10.3 10.4 all-gather
  22.1 53.5 %all_to_all.20 = bf16[4,128,2048]{2,1,0:T(8,128)(2,1)} all-to-all(bf16[4,128,2048]{2,1,0:T(8,128)(2,1)S(1)} %stack.73), channel_id=1, replica_groups=mesh['dp'=8,'tensor'=4] {'tensor'}, dimensions={0} | all-to-all | bytes 4194304 | tf_op jit(solution)/shard_map/all_to_all | solution.py:159
  91.1 38.5 %all-to-all-done = bf16[4,128,2048]{2,1,0:T(8,128)(2,1)} async-done(((bf16[4,128,2048]{2,1,0:T(8,128)(2,1)}), bf16[4,128,2048]{2,1,0:T(8,128)(2,1)}, u32[]{:S(2)}, u32[]{:S(2)}) %all-to-all-start) | async-done | bytes 2097184 | tf_op jit(solution)/shard_map/all_to_all | solution.py:159
  171.1 8.9 all-gather.1
  180.0 44.5 %reduce-scatter.17.cloned.1.call-done = f32[128,2048]{1,0:T(8,128)} async-done(((f32[512,2048]{1,0:T(8,128)}), f32[128,2048]{1,0:T(8,128)}) %reduce-scatter.17.cloned.1.call-update) | async-done | bytes 1048592 | tf_op jit(solution)/shard_map/reduce_scatter | solution.py:168
  224.5 79.5 %reduce-scatter.13.cloned.1.call-done = f32[128,2048]{1,0:T(8,128)} async-done(((f32[512,2048]{1,0:T(8,128)}), f32[128,2048]{1,0:T(8,128)}) %reduce-scatter.13.cloned.1.call-update) | async-done | bytes 1048592 | tf_op jit(solution)/shard_map/reduce_scatter | solution.py:168
  313.1 61.3 %all-gather.15.cloned.1.call-done = bf16[2048,2,1408]{2,0,1:T(8,128)(2,1)} async-done(((bf16[256,2,1408]{2,0,1:T(8,128)(2,1)}), bf16[2048,2,1408]{2,0,1:T(8,128)(2,1)}) %all-gather.15.cloned.1.call-update) | async-done | bytes 11534352 | tf_op jit(solution)/shard_map/all_gather | solution.py:207
  374.4 15.2 copy.87
  389.6 11.9 fusion.2
  401.5 20.6 %all-gather.19.cloned.1.call-done = bf16[512,2048]{1,0:T(8,128)(2,1)} async-done(((bf16[128,2048]{1,0:T(8,128)(2,1)}), bf16[512,2048]{1,0:T(8,128)(2,1)}) %all-gather.19.cloned.1.call-update) | async-done | bytes 2097168 | tf_op jit(solution)/shard_map/all_gather | solution.py:164
  422.1 43.9 %all-gather.17.cloned.1.call-done = bf16[2048,1408]{1,0:T(8,128)(2,1)} async-done(((bf16[256,1408]{1,0:T(8,128)(2,1)}), bf16[2048,1408]{1,0:T(8,128)(2,1)}) %all-gather.17.cloned.1.call-update) | async-done | bytes 5767184 | tf_op jit(solution)/shard_map/all_gather | solution.py:208
  466.0 9.0 multiply_bitcast_fusion.3
  476.6 10.4 convolution_bitcast_fusion.1
  487.0 76.9 %reduce-scatter.21.cloned.1.call-done = f32[128,2048]{1,0:T(8,128)} async-done(((f32[512,2048]{1,0:T(8,128)}), f32[128,2048]{1,0:T(8,128)}) %reduce-scatter.21.cloned.1.call-update) | async-done | bytes 1048592 | tf_op jit(solution)/shard_map/reduce_scatter | solution.py:177
  573.2 81.5 %all-to-all-done.3 = bf16[4,128,2048]{2,1,0:T(8,128)(2,1)} async-done(((bf16[4,128,2048]{2,1,0:T(8,128)(2,1)}), bf16[4,128,2048]{2,1,0:T(8,128)(2,1)}, u32[]{:S(2)}, u32[]{:S(2)}) %all-to-all-start.3) | async-done | bytes 2097184 | tf_op jit(solution)/shard_map/all_to_all | solution.py:159
  654.7 11.8 fusion
  666.5 9.0 multiply_bitcast_fusion.1
  677.0 10.3 convolution_bitcast_fusion
  712.6 49.9 %reduce-scatter.25.cloned.1.call-done = f32[128,2048]{1,0:T(8,128)} async-done(((f32[512,2048]{1,0:T(8,128)}), f32[128,2048]{1,0:T(8,128)}) %reduce-scatter.25.cloned.1.call-update) | async-done | bytes 1048592 | tf_op jit(solution)/shard_map/reduce_scatter | solution.py:177
  764.0 78.1 %reduce-scatter.15.cloned.1.call-done = f32[128,2048]{1,0:T(8,128)} async-done(((f32[512,2048]{1,0:T(8,128)}), f32[128,2048]{1,0:T(8,128)}) %reduce-scatter.15.cloned.1.call-update) | async-done | bytes 1048592 | tf_op jit(solution)/shard_map/reduce_scatter | solution.py:168
  842.1 79.5 %reduce-scatter.19.cloned.1.call-done = f32[128,2048]{1,0:T(8,128)} async-done(((f32[512,2048]{1,0:T(8,128)}), f32[128,2048]{1,0:T(8,128)}) %reduce-scatter.19.cloned.1.call-update) | async-done | bytes 1048592 | tf_op jit(solution)/shard_map/reduce_scatter | solution.py:168
  939.6 33.7 %all-gather.21.cloned.1.call-done = bf16[512,2048]{1,0:T(8,128)(2,1)} async-done(((bf16[128,2048]{1,0:T(8,128)(2,1)}), bf16[512,2048]{1,0:T(8,128)(2,1)}) %all-gather.21.cloned.1.call-update) | async-done | bytes 2097168 | tf_op jit(solution)/shard_map/all_gather | solution.py:164
  988.8 31.1 %all-gather.25.cloned.1.call-done = bf16[512,2048]{1,0:T(8,128)(2,1)} async-done(((bf16[128,2048]{1,0:T(8,128)(2,1)}), bf16[512,2048]{1,0:T(8,128)(2,1)}) %all-gather.25.cloned.1.call-update) | async-done | bytes 2097168 | tf_op jit(solution)/shard_map/all_gather | solution.py:164
  1075.7 13.4 fusion.21
  1092.1 16.8 %convolution_add_fusion = f32[2048,2,1408]{2,0,1:T(8,128)} fusion(f32[2048,2,1408]{2,0,1:T(8,128)} %fusion.21, bf16[512,2048,1]{1,0,2:T(8,128)(2,1)} %bitcast.50, bf16[512,2,1408]{0,2,1:T(8,128)(2,1)} %copy.110), kind=kOutput, calls=%fused_computation | convolution fusion | flops 5911347200 | bytes 51118080 | tf_op jit(solution)/shard_map/dot_general | solution.py:146
  1123.0 45.6 %reduce-scatter.29.cloned.1.call-done = f32[256,1,640]{2,0,1:T(8,128)} async-done(((f32[2048,1,640]{2,0,1:T(8,128)}), f32[256,1,640]{2,0,1:T(8,128)}) %reduce-scatter.29.cloned.1.call-update) | async-done | bytes 655376 | tf_op jit(solution)/shard_map/reduce_scatter | solution.py:291
  1171.2 76.4 %reduce-scatter.27.cloned.1.call-done = f32[128,2048]{1,0:T(8,128)} async-done(((f32[512,2048]{1,0:T(8,128)}), f32[128,2048]{1,0:T(8,128)}) %reduce-scatter.27.cloned.1.call-update) | async-done | bytes 1048592 | tf_op jit(solution)/shard_map/reduce_scatter | solution.py:177
  1247.6 79.5 %reduce-scatter.23.cloned.1.call-done = f32[128,2048]{1,0:T(8,128)} async-done(((f32[512,2048]{1,0:T(8,128)}), f32[128,2048]{1,0:T(8,128)}) %reduce-scatter.23.cloned.1.call-update) | async-done | bytes 1048592 | tf_op jit(solution)/shard_map/reduce_scatter | solution.py:177
  1329.2 23.7 %all-reduce.2 = (f32[2048]{0:T(1024)S(1)}, f32[2048]{0:T(1024)S(1)}) all-reduce(f32[2048]{0:T(1024)S(1)} %add.202, f32[2048]{0:T(1024)S(1)} %add.206), channel_id=10, replica_groups=mesh['dp'=8,'tensor'=4] {'dp'}, use_global_device_ids=true, to_apply=%region_26.27.clone | all-reduce | flops 4096 | bytes 32768
  1353.0 12.0 all-reduce.3
  1368.9 108.7 %reduce-scatter.33.cloned.1.call-done = f32[256,2,1408]{2,0,1:T(8,128)} async-done(((f32[2048,2,1408]{2,0,1:T(8,128)}), f32[256,2,1408]{2,0,1:T(8,128)}) %reduce-scatter.33.cloned.1.call-update) | async-done | bytes 2883600 | tf_op jit(solution)/shard_map/reduce_scatter | solution.py:291
  1483.2 49.4 %reduce-scatter.31.cloned.1.call-done = f32[256,512]{1,0:T(8,128)} async-done(((f32[2048,512]{1,0:T(8,128)}), f32[256,512]{1,0:T(8,128)}) %reduce-scatter.31.cloned.1.call-update) | async-done | bytes 524304 | tf_op jit(solution)/shard_map/reduce_scatter | solution.py:291
  (332 shorter events, 228.4 us)
Async XLA Ops:
  7.2 77.2 %all-gather.11.cloned.1.call-start = ((), (), s32[]{:S(2)}) async-start(), calls=%async_computation.16 | async-start | bytes 2949120 | tf_op jit(solution)/shard_map/all_gather | solution.py:204
  77.2 52.4 %all-to-all-start = ((bf16[4,128,2048]{2,1,0:T(8,128)(2,1)}), bf16[4,128,2048]{2,1,0:T(8,128)(2,1)}, u32[]{:S(2)}, u32[]{:S(2)}) async-start(bf16[4,128,2048]{2,1,0:T(8,128)(2,1)} %stack.69), calls=%async_computation | async-start | bytes 4194304 | tf_op jit(solution)/shard_map/all_to_all | solution.py:159
  81.7 62.7 %all-gather.13.cloned.1.call-start = ((), (), s32[]{:S(2)}) async-start(), calls=%async_computation.17 | async-start | bytes 2359296 | tf_op jit(solution)/shard_map/all_gather | solution.py:205
  82.4 142.1 %reduce-scatter.17.cloned.1.call-start = ((), (), s32[]{:S(2)}) async-start(), calls=%async_computation.22 | async-start | bytes 5242880 | tf_op jit(solution)/shard_map/reduce_scatter | solution.py:168
  149.4 154.6 %reduce-scatter.13.cloned.1.call-start = ((), (), s32[]{:S(2)}) async-start(), calls=%async_computation.18 | async-start | bytes 5242880 | tf_op jit(solution)/shard_map/reduce_scatter | solution.py:168
  164.8 209.6 %all-gather.15.cloned.1.call-start = ((), (), s32[]{:S(2)}) async-start(), calls=%async_computation.19 | async-start | bytes 12976128 | tf_op jit(solution)/shard_map/all_gather | solution.py:207
  167.5 254.6 %all-gather.19.cloned.1.call-start = ((), (), s32[]{:S(2)}) async-start(), calls=%async_computation.24 | async-start | bytes 2621440 | tf_op jit(solution)/shard_map/all_gather | solution.py:164
  170.3 295.7 %all-gather.17.cloned.1.call-start = ((), (), s32[]{:S(2)}) async-start(), calls=%async_computation.20 | async-start | bytes 6488064 | tf_op jit(solution)/shard_map/all_gather | solution.py:208
  308.5 81.1 %all-to-all-start.1 = ((bf16[4,128,2048]{2,1,0:T(8,128)(2,1)}), bf16[4,128,2048]{2,1,0:T(8,128)(2,1)S(1)}, u32[]{:S(2)}, u32[]{:S(2)}) async-start(bf16[4,128,2048]{2,1,0:T(8,128)(2,1)} %stack.70), calls=%async_computation.2 | async-start | bytes 4194304 | tf_op jit(solution)/shard_map/all_to_all | solution.py:159
  312.7 251.2 %reduce-scatter.21.cloned.1.call-start = ((), (), s32[]{:S(2)}) async-start(), calls=%async_computation.25 | async-start | bytes 5242880 | tf_op jit(solution)/shard_map/reduce_scatter | solution.py:177
  487.0 77.0 %copy-start.7 = (f32[128,2048]{1,0:T(8,128)S(1)}, f32[128,2048]{1,0:T(8,128)}, u32[]{:S(2)}) copy-start(f32[128,2048]{1,0:T(8,128)} %get-tuple-element.69) | copy-start | bytes 3145732
  567.7 87.0 %all-to-all-start.3 = ((bf16[4,128,2048]{2,1,0:T(8,128)(2,1)}), bf16[4,128,2048]{2,1,0:T(8,128)(2,1)}, u32[]{:S(2)}, u32[]{:S(2)}) async-start(bf16[4,128,2048]{2,1,0:T(8,128)(2,1)} %stack.74), calls=%async_computation.6 | async-start | bytes 4194304 | tf_op jit(solution)/shard_map/all_to_all | solution.py:159
  572.2 94.3 %all-gather.23.cloned.1.call-start = ((), (), s32[]{:S(2)}) async-start(), calls=%async_computation.28 | async-start | bytes 2621440 | tf_op jit(solution)/shard_map/all_gather | solution.py:164
  572.9 189.6 %reduce-scatter.25.cloned.1.call-start = ((), (), s32[]{:S(2)}) async-start(), calls=%async_computation.29 | async-start | bytes 5242880 | tf_op jit(solution)/shard_map/reduce_scatter | solution.py:177
  687.4 154.7 %reduce-scatter.15.cloned.1.call-start = ((), (), s32[]{:S(2)}) async-start(), calls=%async_computation.21 | async-start | bytes 5242880 | tf_op jit(solution)/shard_map/reduce_scatter | solution.py:168
  699.9 221.7 %reduce-scatter.19.cloned.1.call-start = ((), (), s32[]{:S(2)}) async-start(), calls=%async_computation.23 | async-start | bytes 5242880 | tf_op jit(solution)/shard_map/reduce_scatter | solution.py:168
  712.5 209.1 %copy-start.20 = (f32[128,2048]{1,0:T(8,128)S(1)}, f32[128,2048]{1,0:T(8,128)}, u32[]{:S(2)}) copy-start(f32[128,2048]{1,0:T(8,128)} %reduce-scatter.21.cloned.1.call-done) | copy-start | bytes 3145732
  712.6 260.8 %all-gather.21.cloned.1.call-start = ((), (), s32[]{:S(2)}) async-start(), calls=%async_computation.26 | async-start | bytes 2621440 | tf_op jit(solution)/shard_map/all_gather | solution.py:164
  927.0 92.8 %all-gather.25.cloned.1.call-start = ((), (), s32[]{:S(2)}) async-start(), calls=%async_computation.30 | async-start | bytes 2621440 | tf_op jit(solution)/shard_map/all_gather | solution.py:164
  927.6 192.2 %reduce-scatter.35.cloned.1.call-start = ((), (), s32[]{:S(2)}) async-start(), calls=%async_computation.35 | async-start | bytes 12976128 | tf_op jit(solution)/shard_map/reduce_scatter | solution.py:291
  939.1 229.5 %reduce-scatter.29.cloned.1.call-start = ((), (), s32[]{:S(2)}) async-start(), calls=%async_computation.32 | async-start | bytes 5898240 | tf_op jit(solution)/shard_map/reduce_scatter | solution.py:291
  1059.2 188.4 %reduce-scatter.27.cloned.1.call-start = ((), (), s32[]{:S(2)}) async-start(), calls=%async_computation.31 | async-start | bytes 5242880 | tf_op jit(solution)/shard_map/reduce_scatter | solution.py:177
  1064.8 262.3 %reduce-scatter.23.cloned.1.call-start = ((), (), s32[]{:S(2)}) async-start(), calls=%async_computation.27 | async-start | bytes 5242880 | tf_op jit(solution)/shard_map/reduce_scatter | solution.py:177
  1070.8 406.8 %reduce-scatter.33.cloned.1.call-start = ((), (), s32[]{:S(2)}) async-start(), calls=%async_computation.34 | async-start | bytes 25952256 | tf_op jit(solution)/shard_map/reduce_scatter | solution.py:291
  1109.0 423.6 %reduce-scatter.31.cloned.1.call-start = ((), (), s32[]{:S(2)}) async-start(), calls=%async_computation.33 | async-start | bytes 4718592 | tf_op jit(solution)/shard_map/reduce_scatter | solution.py:291
  1119.8 207.3 %copy-start.3 = (f32[2,128,2048]{2,1,0:T(8,128)S(1)}, f32[2,128,2048]{2,1,0:T(8,128)}, u32[]{:S(2)}) copy-start(f32[2,128,2048]{2,1,0:T(8,128)} %param.9) | copy-start | bytes 6291460
  1119.8 207.3 %copy-start.67 = (f32[8,1,256]{2,1,0:T(1,128)S(1)}, f32[8,1,256]{2,1,0:T(1,128)}, u32[]{:S(2)}) copy-start(f32[8,1,256]{2,1,0:T(1,128)} %copy-done.66) | copy-start | bytes 24580
  1119.8 207.3 %copy-start.74 = (f32[128]{0:T(128)S(1)}, f32[128]{0:T(128)}, u32[]{:S(2)}) copy-start(f32[128]{0:T(128)} %copy-done.73) | copy-start | bytes 1540
  1119.8 207.3 %copy-start.76 = (f32[128]{0:T(128)S(1)}, f32[128]{0:T(128)}, u32[]{:S(2)}) copy-start(f32[128]{0:T(128)} %copy-done.75) | copy-start | bytes 1540
  1123.0 242.0 %copy-start.80 = (f32[128]{0:T(128)S(1)}, f32[128]{0:T(128)}, u32[]{:S(2)}) copy-start(f32[128]{0:T(128)} %get-tuple-element.97) | copy-start | bytes 1540
  1123.0 242.0 %copy-start.81 = (f32[128]{0:T(128)S(1)}, f32[128]{0:T(128)}, u32[]{:S(2)}) copy-start(f32[128]{0:T(128)} %get-tuple-element.118) | copy-start | bytes 1540
  1247.6 117.4 %copy-start.23 = (f32[128,2048]{1,0:T(8,128)S(1)}, f32[128,2048]{1,0:T(8,128)}, u32[]{:S(2)}) copy-start(f32[128,2048]{1,0:T(8,128)} %reduce-scatter.27.cloned.1.call-done) | copy-start | bytes 3145732
  (82 other events, 617.3 us)
Sparse Core Ops, SparseCore 0:
  9.9 32.6 all-gather.10
  84.4 28.2 all-gather.12
  149.5 74.9 reduce-scatter.16
  226.7 77.2 reduce-scatter.12
  306.3 68.0 all-gather.14
  376.4 45.6 all-gather.18
  424.0 41.9 all-gather.16
  487.1 76.7 reduce-scatter.20
  575.1 74.1 all-gather.22
  687.5 74.9 reduce-scatter.24
  764.8 77.2 reduce-scatter.14
  844.2 77.2 reduce-scatter.18
  927.1 46.1 all-gather.20
  975.3 44.4 all-gather.24
  1023.2 85.6 reduce-scatter.34
  1112.1 56.4 reduce-scatter.28
  1170.8 76.7 reduce-scatter.26
  1249.8 77.2 reduce-scatter.22
  1330.7 146.8 reduce-scatter.32
  1481.4 51.1 reduce-scatter.30
